TPU v7x, 16 devices: a whole 2x2x2 slice. The times are simulated.
16 devices in a mesh: pp: 2 (over z), dp: 8 (over y, x, core).
Axes of the slice: x: 2, y: 2, z: 2, core: 2. Of those that a mesh axis runs over, the one named last changes fastest.
Arguments:
- w_in: bfloat16 [2, 16, 256, 1024], P('pp')
- w_out: bfloat16 [2, 16, 1024, 256], P('pp')
- x_saved: bfloat16 [2, 2, 16, 4096, 256], P('pp', None, None, 'dp')
- h_saved: bfloat16 [2, 2, 16, 4096, 1024], P('pp', None, None, 'dp')
- dy_in: bfloat16 [2, 4096, 256], P('pp', 'dp')
- acc_in: float32 [2, 8, 16, 256, 1024], P('pp', 'dp')
- acc_out: float32 [2, 8, 16, 1024, 256], P('pp', 'dp')
Outputs:
- output 1: float32 [2, 16, 256, 1024], P('pp')
- output 2: float32 [2, 16, 1024, 256], P('pp')
- output 3: bfloat16 [2, 4096, 256], P('pp', 'dp')
All inputs are finite; a program needn't handle non-finite values.
Results may differ from a plain program's by a relative error of at most 0.0117373.
Values are sent between devices in bfloat16 or wider.
A program may use at most 1 GiB of HBM per device.

v0:
```python
import functools
import jax
import jax.numpy as jnp
from jax import lax
from jax.sharding import PartitionSpec as P


def layer_backward(w_first, w_second, x_in, h_pre, cot_in):
    act_val, act_vjp = jax.vjp(jax.nn.gelu, h_pre.astype(jnp.float32))
    act_bf = act_val.astype(jnp.bfloat16)
    d_act = lax.dot_general(cot_in, w_second, (((1,), (1,)), ((), ())), preferred_element_type=jnp.float32)
    d_pre = act_vjp(d_act)[0].astype(jnp.bfloat16)
    grad_first = lax.dot_general(x_in, d_pre, (((0,), (0,)), ((), ())), preferred_element_type=jnp.float32)
    grad_second = lax.dot_general(act_bf, cot_in, (((0,), (0,)), ((), ())), preferred_element_type=jnp.float32)
    back_sum = lax.dot_general(d_pre, w_first, (((1,), (1,)), ((), ())), preferred_element_type=jnp.float32)
    cot_out = (cot_in.astype(jnp.float32) + back_sum).astype(jnp.bfloat16)
    return cot_out, grad_first, grad_second


def solution(mesh):
    stages = mesh.shape['pp']
    replicas = mesh.shape['dp']
    down_pairs = [(sender, sender - 1) for sender in range(1, stages)]

    def device_fn(w_in, w_out, x_saved, h_saved, dy_in, acc_in, acc_out):
        stage_id = lax.axis_index('pp')
        w_first = w_in[0]
        w_second = w_out[0]
        layers = w_first.shape[0]
        x_local = x_saved[0]
        h_local = h_saved[0]

        def backward_slot(slot_id, operands):
            cot_cur, acc_first, acc_second = operands
            new_first = list(acc_first)
            new_second = list(acc_second)
            x_slot = lax.dynamic_index_in_dim(x_local, slot_id, 0, keepdims=False)
            h_slot = lax.dynamic_index_in_dim(h_local, slot_id, 0, keepdims=False)
            for layer_id in reversed(range(layers)):
                cot_cur, grad_first, grad_second = layer_backward(w_first[layer_id], w_second[layer_id], x_slot[layer_id], h_slot[layer_id], cot_cur)
                new_first[layer_id] = new_first[layer_id] + grad_first
                new_second[layer_id] = new_second[layer_id] + grad_second
            return cot_cur, new_first, new_second

        def run_step(slot_id, loop_state):
            cot_cur, acc_first, acc_second, dx_all = loop_state
            cot_cur, acc_first, acc_second = lax.cond(stage_id + slot_id < stages, functools.partial(backward_slot, slot_id), lambda operands: operands, (cot_cur, acc_first, acc_second))
            dx_all = lax.dynamic_update_index_in_dim(dx_all, cot_cur, slot_id, 0)
            return cot_cur, acc_first, acc_second, dx_all

        def loop_body(slot_id, loop_state):
            cot_cur, acc_first, acc_second, dx_all = run_step(slot_id, loop_state)
            cot_next = lax.ppermute(cot_cur, 'pp', perm=down_pairs)
            return cot_next, acc_first, acc_second, dx_all

        acc_first = [acc_in[0, 0, layer_id] for layer_id in range(layers)]
        acc_second = [acc_out[0, 0, layer_id] for layer_id in range(layers)]
        dx_all = jnp.zeros((stages,) + dy_in.shape[1:], jnp.bfloat16)
        loop_state = lax.fori_loop(0, stages - 1, loop_body, (dy_in[0], acc_first, acc_second, dx_all))
        final_state = run_step(stages - 1, loop_state)
        sum_first = lax.psum(jnp.stack(final_state[1]).astype(jnp.bfloat16), 'dp')
        sum_second = lax.psum(jnp.stack(final_state[2]).astype(jnp.bfloat16), 'dp')
        grad_in = (sum_first.astype(jnp.float32) / replicas)[None]
        grad_out = (sum_second.astype(jnp.float32) / replicas)[None]
        from_first = jnp.where(stage_id == 0, final_state[3], jnp.zeros_like(final_state[3]))
        dx_out = lax.psum_scatter(from_first, 'pp', scatter_dimension=0, tiled=True)
        return grad_in, grad_out, dx_out

    return jax.shard_map(device_fn, mesh=mesh, in_specs=(P('pp'), P('pp'), P('pp', None, None, 'dp'), P('pp', None, None, 'dp'), P('pp', 'dp'), P('pp', 'dp'), P('pp', 'dp')), out_specs=(P('pp'), P('pp'), P('pp', 'dp')), check_vma=False)
```

profile of v0, /device:TPU:0, one launch (start us, length us, event | category | flops | bytes accessed | tf_op | source)
XLA Modules:
  0.0 658.4 jit_solution(13308845718445576065)
XLA Ops:
  8.0 11.1 %fusion.961 = (f32[1,1,1,256,1024]{4,3,2,1,0:T(8,128)}, f32[1,1,1,256,1024]{4,3,2,1,0:T(8,128)S(1)}, f32[1,1,1,256,1024]{4,3,2,1,0:T(8,128)S(1)}, f32[1,1,1,256,...) fusion(f32[1,1,16,256,1024]{4,3,2,1,0:T(8,128)} %param.16), kind=kLoop, calls=%fused_computation.1268 | loop fusion | bytes 33554432 | tf_op jit(solution)/shard_map/slice | solution.py:56
  53.3 12.6 %slice_bitcast_fusion = (f32[1024,256]{1,0:T(8,128)}, f32[1024,256]{1,0:T(8,128)}, f32[1024,256]{1,0:T(8,128)}, f32[1024,256]{1,0:T(8,128)}, f32[1024,256]{1,0:T...) fusion(f32[1,1,16,1024,256]{4,3,2,1,0:T(8,128)} %param.17), kind=kLoop, calls=%fused_computation.1219 | loop fusion | bytes 33554432 | tf_op jit(solution)/shard_map/squeeze | solution.py:57
  66.0 125.5 %conditional.2 = (bf16[512,256]{1,0:T(8,128)(2,1)}, f32[256,1024]{0,1:T(8,128)}, f32[256,1024]{0,1:T(8,128)}, f32[256,1024]{0,1:T(8,128)}, f32[256,1024]{0,1:T(8...) conditional(s32[]{:T(128)} %convert_element_type.592, ...), branch_computations={%region_0.1_spmd, %region_1.2_spmd} | conditional | flops 17454596096 | bytes 539495296 | solution.py:47
  66.0 3.1 fusion.63
  70.8 3.0 fusion.60
  81.0 2.9 fusion.51
  84.4 2.9 fusion.48
  88.1 2.9 fusion.45
  91.5 2.9 fusion.42
  94.9 2.9 fusion.39
  98.4 2.9 fusion.36
  101.8 2.9 fusion.33
  105.2 3.1 fusion.30
  108.9 2.9 fusion.27
  112.3 2.9 fusion.24
  115.8 3.0 fusion.21
  119.3 3.1 fusion.18
  192.7 9.6 %collective-permute-done = bf16[512,256]{1,0:T(8,128)(2,1)} collective-permute-done((bf16[512,256]{1,0:T(8,128)(2,1)}, bf16[512,256]{1,0:T(8,128)(2,1)}, u32[]{:S(2)}, u32[]{:S(2)}) %collective-permute-start) | collective-permute-done | bytes 262176 | tf_op jit(solution)/shard_map/while/body/eval_jaxpr/ppermute | solution.py:53
  202.3 184.4 %conditional.3 = (bf16[1,1024,256]{2,1,0:T(8,128)(2,1)}, bf16[1,1024,256]{2,1,0:T(8,128)(2,1)}, bf16[1,1024,256]{2,1,0:T(8,128)(2,1)}, bf16[1,1024,256]{2,1,0:T(...) conditional(s32[]{:T(128)} %convert_element_type.591, ...), branch_computations={%region_2.3_spmd, %region_3.4_spmd} | conditional | flops 17462984704 | bytes 461376064 | solution.py:47
  202.7 3.2 fusion.511
  208.0 3.0 fusion.508
  215.0 2.9 fusion.502
  222.0 2.9 fusion.496
  225.6 2.9 fusion.493
  229.1 2.9 fusion.490
  236.0 2.9 fusion.484
  242.9 3.1 fusion.478
  246.6 2.9 fusion.475
  253.5 2.9 fusion.469
  260.9 3.2 fusion.672
  274.5 3.9 fusion.687
  282.7 3.5 fusion.686
  290.6 3.5 fusion.685
  298.5 3.6 fusion.684
  306.4 3.6 fusion.683
  314.3 3.5 fusion.682
  322.1 3.6 fusion.681
  330.1 3.6 fusion.680
  338.2 3.6 fusion.679
  346.1 3.5 fusion.678
  354.0 3.6 fusion.677
  361.9 3.5 fusion.676
  369.7 3.5 fusion.675
  377.7 3.2 fusion.674
  380.8 3.2 fusion.673
  419.4 208.2 %all-reduce.3.cloned.1.call-done = (bf16[16,256,1024]{2,1,0:T(8,128)(2,1)}, bf16[16,1024,256]{2,1,0:T(8,128)(2,1)}) async-done(((bf16[16,256,1024]{2,1,0:T(8,128)(2,1)}, bf16[16,1024,256]{2,1,0:T(8,128)(2,1)}), (bf16[16,256,1024]{2,1,0:T(8,128)(2,1)}, bf16[16,1024,256]{2,1,0:T(8,128)(2,1)})) %all-reduce.3.cloned.1.call-update) | async-done | bytes 16777232 | tf_op jit(solution)/shard_map/psum | solution.py:61
  627.5 11.2 %multiply_bitcast_fusion = f32[1,16,1024,256]{3,2,1,0:T(8,128)} fusion(bf16[16,1024,256]{2,1,0:T(8,128)(2,1)} %get-tuple-element.1062), kind=kLoop, calls=%fused_computation.1217 | loop fusion | flops 8388608 | bytes 25165824 | tf_op jit(solution)/shard_map/broadcast_in_dim | solution.py:64
  638.7 12.0 %multiply_bitcast_fusion.1 = f32[1,16,256,1024]{3,2,1,0:T(8,128)} fusion(bf16[16,256,1024]{2,1,0:T(8,128)(2,1)} %get-tuple-element.1061), kind=kLoop, calls=%fused_computation.1218 | loop fusion | flops 8388608 | bytes 25165824 | tf_op jit(solution)/shard_map/broadcast_in_dim | solution.py:63
  (525 shorter events, 247.2 us)
Async XLA Ops:
  8.0 619.5 %all-reduce.3.cloned.1.call-start = ((), (), s32[]{:S(2)}) async-start(), calls=%async_computation.2 | async-start | bytes 33554432 | tf_op jit(solution)/shard_map/psum | solution.py:61
  53.3 12.6 %copy-start.99 = (bf16[1,512,256]{2,1,0:T(8,128)(2,1)S(1)}, bf16[1,512,256]{2,1,0:T(8,128)(2,1)}, u32[]{:S(2)}) copy-start(bf16[1,512,256]{2,1,0:T(8,128)(2,1)} %param.15) | copy-start | bytes 786436
  66.0 4.8 copy-start.146
  69.1 4.7 slice-start.2
  115.8 6.6 %slice-start = ((s8[8388608]{0:T(1024)(128)(4,1)}), s8[4194304]{0:T(1024)(128)(4,1)S(1)}, s32[]{:S(2)}) async-start(s8[8388608]{0:T(1024)(128)(4,1)} %bitcast.992), calls=%async_computation.3 | async-start | bytes 8388608 | tf_op jit(solution)/shard_map/while/body/eval_jaxpr/cond
  123.1 3.7 copy-start.43
  130.4 4.8 copy-start.91
  131.1 4.1 copy-start.41
  135.2 4.3 copy-start.88
  135.9 3.7 copy-start.38
  139.6 4.3 copy-start.85
  143.9 4.3 copy-start.82
  148.2 4.3 copy-start.79
  152.6 4.3 copy-start.76
  156.9 4.3 copy-start.73
  161.2 4.3 copy-start.70
  165.6 4.1 copy-start.67
  169.7 4.3 copy-start.64
  170.4 3.6 copy-start.10
  174.1 4.3 copy-start.61
  178.4 4.0 copy-start.58
  182.4 4.0 copy-start.55
  186.4 4.0 copy-start.51
  191.4 10.9 %copy-start.97 = (bf16[1,512,256]{2,1,0:T(8,128)(2,1)}, bf16[1,512,256]{2,1,0:T(8,128)(2,1)S(1)}, u32[]{:S(2)}) copy-start(bf16[1,512,256]{2,1,0:T(8,128)(2,1)S(1)} %get-tuple-element.978) | copy-start | bytes 786436
  191.4 10.9 %collective-permute-start = (bf16[512,256]{1,0:T(8,128)(2,1)}, bf16[512,256]{1,0:T(8,128)(2,1)}, u32[]{:S(2)}, u32[]{:S(2)}) collective-permute-start(bf16[512,256]{1,0:T(8,128)(2,1)} %get-tuple-element.879), channel_id=1, source_target_pairs={{8,0},{9,1},{10,2},{11,3},{12,4},{13,5},{14,6},{15,7}} | collective-permute-start | bytes 786440 | tf_op jit(solution)/shard_map/while/body/eval_jaxpr/ppermute | solution.py:53
  202.7 5.3 copy-start.147
  206.0 5.1 copy-start.117
  206.0 5.1 slice-start.4
  242.4 3.7 copy-start.137
  274.5 3.9 copy-start.39
  274.5 3.9 copy-start.144
  278.4 4.3 copy-start.195
  286.3 4.3 copy-start.191
  294.1 4.4 copy-start.187
  302.1 4.3 copy-start.183
  309.9 4.3 copy-start.179
  317.8 4.3 copy-start.175
  325.7 4.4 copy-start.171
  333.7 4.5 copy-start.167
  341.7 4.3 copy-start.163
  349.6 4.4 copy-start.159
  357.6 4.4 copy-start.155
  365.4 4.3 copy-start.153
  373.3 4.4 copy-start.53
  373.3 4.4 copy-start.151
  399.4 4.6 copy-start.116
  404.1 10.0 %copy-start.45 = (bf16[16,1024,256]{2,1,0:T(8,128)(2,1)}, bf16[16,1024,256]{2,1,0:T(8,128)(2,1)S(1)}, u32[]{:S(2)}) copy-start(bf16[16,1024,256]{2,1,0:T(8,128)(2,1)S(1)} %constant_dynamic-update-slice_fusion.16) | copy-start | bytes 25165828
  416.6 234.1 %reduce-scatter.2.cloned.1.call-start = ((), (), s32[]{:S(2)}) async-start(), calls=%async_computation.1 | async-start | bytes 786432 | tf_op jit(solution)/shard_map/reduce_scatter | solution.py:66
  (136 other events, 387.1 us)
Sparse Core Ops, SparseCore 0:
  416.7 210.7 all-reduce.2
Sparse Core Ops, SparseCore 1:
  419.9 13.5 reduce-scatter.1
where the time goes:
time: 668 us; the launch traced here: 658 us
  matrix products  257 us (38%)
  waiting for transfers between devices  218 us (33%)
  local copies, waits for them, and re-layouts  138 us (21%)
  other arithmetic  24.9 us (4%)
  between operations  16 us (2%)
    psum x1, waiting for transfers between devices, device_fn(): sum_first = lax.psum(jnp.stack(final_state[1]).astype(jnp.bfloat16), 'dp')  208 us
    dot_general x32, matrix products, layer_backward(): lax.dot_general(act_bf, cot_in, (((0,), (0,)), ((), ())), preferred_eleme...  95.5 us
    dot_general x32, matrix products, layer_backward(): lax.dot_general(cot_in, w_second, (((1,), (1,)), ((), ())), preferred_ele...  94.8 us
    unnamed x88, local copies, waits for them, and re-layouts  63.9 us
    cond x337, local copies, waits for them, and re-layouts  50 us
    dot_general x32, matrix products, layer_backward(): lax.dot_general(x_in, d_pre, (((0,), (0,)), ((), ())), preferred_element_...  46.7 us
    dot_general x32, matrix products, layer_backward(): lax.dot_general(d_pre, w_first, (((1,), (1,)), ((), ())), preferred_eleme...  19.8 us
  transfers between devices with their start and end apart: 3, of which 2 were waited for; matrix products, arithmetic and copies ran while one was open for 4% of the time, Pallas kernels for 0%

commit v1 on v0

v1 whole, which is shorter than its diff:
```python
import functools
import jax
import jax.numpy as jnp
from jax import lax
from jax.experimental import pallas as pl
from jax.experimental.pallas import tpu as pltpu
from jax.sharding import PartitionSpec as P

SUB = 4
LAG = 3
MESH = pl.DeviceIdType.MESH
ROOT_2_PI = 0.7978845608028654
CUBIC = 0.044715
F32 = jnp.float32
BF16 = jnp.bfloat16


def gelu_value(h):
    p = ROOT_2_PI + (ROOT_2_PI * CUBIC) * (h * h)
    s = 0.5 + 0.5 * jnp.tanh(h * p)
    return h * s


def gelu_slope(h):
    h2 = h * h
    p = ROOT_2_PI + (ROOT_2_PI * CUBIC) * h2
    s = 0.5 + 0.5 * jnp.tanh(h * p)
    a = h * s
    q = 2.0 * ROOT_2_PI + (6.0 * ROOT_2_PI * CUBIC) * h2
    return a, s + (a - a * s) * q


def dot_nt(a, b):
    return lax.dot_general(a, b, (((1,), (1,)), ((), ())), preferred_element_type=F32)


def dot_tn(a, b):
    return lax.dot_general(a, b, (((0,), (0,)), ((), ())), preferred_element_type=F32)


def kernel(layers, blk, w1_hbm, w2_hbm, x_hbm, h_hbm, dy_hbm, acc1_hbm, acc2_hbm,
           gi_hbm, go_hbm, dx_hbm, dh_hbm,
           part, from_sib, rs1_in, rs2_in, full, to_sib,
           w1b, w2b, hb, xb, dhb, a1b, a2b, c_save, c_cur, c_sum, z_in,
           sw1, sw2, sh, sx, sdh_in, sdh_out, sa1, sa2, s_misc,
           sib_send, sib_recv, rs1_send, rs1_recv, rs2_send, rs2_recv,
           ag2_send, ag2_recv, ag1_send, ag1_recv, out_local, out_send, out_recv,
           z_send, z_recv):
    pp = lax.axis_index('pp')
    dp = lax.axis_index('dp')
    core = lax.rem(dp, 2)
    bx = lax.rem(lax.div(dp, 2), 2)
    by = lax.div(dp, 4)
    b1 = bx + core * (by - bx)
    b2 = by + core * (bx - by)
    d1 = 2 + 2 * core
    d2 = 4 - 2 * core
    n1 = dp + (1 - 2 * b1) * d1
    n2 = dp + (1 - 2 * b2) * d2
    sib = dp + 1 - 2 * core
    quarter = 2 * b1 + b2
    first = pp == 0
    chunks = layers * SUB
    rows = blk // SUB

    barrier = pltpu.get_barrier_semaphore()
    for peer in ((pp, sib), (pp, n1), (pp, n2), (1 - pp, dp)):
        pl.semaphore_signal(barrier, inc=1, device_id=peer, device_id_type=MESH)
    pl.semaphore_wait(barrier, 4)

    def load_w(layer, slot):
        return (pltpu.make_async_copy(w1_hbm.at[0, layer], w1b.at[slot], sw1.at[slot]),
                pltpu.make_async_copy(w2_hbm.at[0, layer], w2b.at[slot], sw2.at[slot]))

    def load_h(micro, layer, slot):
        return pltpu.make_async_copy(h_hbm.at[0, micro, layer], hb.at[slot], sh.at[slot])

    def load_x(micro, layer, slot):
        return pltpu.make_async_copy(x_hbm.at[0, micro, layer], xb.at[slot], sx.at[slot])

    def load_rest(layer, slot):
        return (pltpu.make_async_copy(acc1_hbm.at[0, 0, layer], a1b.at[slot], sa1.at[slot]),
                pltpu.make_async_copy(acc2_hbm.at[0, 0, layer], a2b.at[slot], sa2.at[slot]),
                pltpu.make_async_copy(dh_hbm.at[layer], dhb.at[2 + slot], sdh_in.at[slot]),
                load_h(0, layer, 2 + slot), load_x(0, layer, slot))

    def load_second(layer, slot):
        return load_w(layer, slot) + (load_h(1, layer, slot), load_x(1, layer, 2 + slot))

    def save_dh(layer, slot):
        return pltpu.make_async_copy(dhb.at[slot], dh_hbm.at[layer], sdh_out.at[slot])

    def start_grad(step):
        layer, slot = layers - 1 - step, lax.rem(step, 2)
        for copy in load_rest(layer, slot):
            copy.start()

        @pl.when(first)
        def _():
            for copy in load_second(layer, slot):
                copy.start()

    def rs1(k):
        half = 2 * (1 - b1)
        return pltpu.make_async_remote_copy(part.at[k, pl.ds(half, 2)], rs1_in.at[k], rs1_send.at[k], rs1_recv.at[k],
                                            device_id=(pp, n1), device_id_type=MESH)

    def rs2(k):
        return pltpu.make_async_remote_copy(part.at[k, 2 * b1 + 1 - b2], rs2_in.at[k], rs2_send.at[k], rs2_recv.at[k],
                                            device_id=(pp, n2), device_id_type=MESH)

    def ag2(k):
        return pltpu.make_async_remote_copy(full.at[k, quarter], full.at[k, quarter], ag2_send.at[k], ag2_recv.at[k],
                                            device_id=(pp, n2), device_id_type=MESH)

    def ag1(k):
        mine = full.at[k, pl.ds(2 * b1, 2)]
        return pltpu.make_async_remote_copy(mine, mine, ag1_send.at[k], ag1_recv.at[k],
                                            device_id=(pp, n1), device_id_type=MESH)

    def swap(step):
        slot = lax.rem(step, 2)
        return pltpu.make_async_remote_copy(to_sib.at[slot], from_sib.at[pl.ds(step * SUB, SUB)],
                                            sib_send.at[slot], sib_recv.at[step],
                                            device_id=(pp, sib), device_id_type=MESH)

    def emit(k):
        layer = layers - 1 - lax.div(k, SUB)
        row = pl.multiple_of(lax.rem(k, SUB) * rows, rows)

        def send(src, dst):
            pltpu.make_async_copy(src, dst, out_local).start()
            pltpu.make_async_remote_copy(src, dst, out_send, out_recv, device_id=(pp, sib), device_id_type=MESH).start()

        @pl.when(core == 0)
        def _():
            for q in range(4):
                send(full.at[k, q], gi_hbm.at[layer, pl.ds(row, rows), pl.ds(q * blk, blk)])

        @pl.when(core == 1)
        def _():
            for q in range(4):
                send(full.at[k, q], go_hbm.at[layer, pl.ds(q * blk + row, rows), :])

    def pump(i):
        def phase(n, body):
            k = i - n * LAG
            pl.when((k >= 0) & (k < chunks))(lambda: body(k))

        def sum0(k):
            @pl.when(lax.rem(k, SUB) == 0)
            def _():
                swap(lax.div(k, SUB)).wait_recv()
            part[k] = part[k] + from_sib[k]

        def sum1(k):
            rs1(k).wait()
            for j in range(2):
                part[k, 2 * b1 + j] = part[k, 2 * b1 + j] + rs1_in[k, j]

        def sum2(k):
            rs2(k).wait()
            full[k, quarter] = part[k, quarter] + rs2_in[k]

        def done2(k):
            ag2(k).wait()
            ag1(k).start()

        def done1(k):
            ag1(k).wait()
            emit(k)

        phase(2, sum2)
        phase(1, sum1)
        phase(0, sum0)
        phase(3, done2)
        phase(2, lambda k: ag2(k).start())
        phase(1, lambda k: rs2(k).start())
        phase(0, lambda k: rs1(k).start())
        phase(4, done1)

    def cols(f):
        return slice(f * blk, (f + 1) * blk)

    first_c = pltpu.make_async_copy(dy_hbm.at[0], c_cur, s_misc)
    first_c.start()
    for copy in load_w(layers - 1, 0) + (load_h(0, layers - 1, 0),):
        copy.start()
    first_c.wait()

    def chain(c, hs, ws, with_grads):
        total = None
        for f in range(4):
            h = hb[hs, :, cols(f)].astype(F32)
            a, slope = gelu_slope(h)
            d = (dot_nt(c, w2b[ws, cols(f), :]) * slope).astype(BF16)
            with_grads(f, a, d)
            back = dot_nt(d, w1b[ws, :, cols(f)])
            total = back if total is None else total + back
        return (c.astype(F32) + total).astype(BF16)

    def chain_step(i, carry):
        layer, slot = layers - 1 - i, lax.rem(i, 2)
        for copy in load_w(layer, slot) + (load_h(0, layer, slot),):
            copy.wait()

        @pl.when(i + 1 < layers)
        def _():
            for copy in load_w(layer - 1, 1 - slot) + (load_h(0, layer - 1, 1 - slot),):
                copy.start()

        @pl.when(i + 1 == layers)
        def _():
            start_grad(0)

        @pl.when(i >= 2)
        def _():
            save_dh(layer + 2, slot).wait()

        c = c_cur[...]
        c_save[layer] = c

        def keep(f, a, d):
            dhb[slot, :, cols(f)] = d

        c_cur[...] = chain(c, slot, slot, keep)
        save_dh(layer, slot).start()
        return carry

    lax.fori_loop(0, layers, chain_step, 0)

    down = pltpu.make_async_remote_copy(c_cur, z_in, z_send, z_recv, device_id=(1 - pp, dp), device_id_type=MESH)
    keep_dx = pltpu.make_async_copy(c_cur, dx_hbm, s_misc)

    @pl.when(pp == 1)
    def _():
        down.start()
        down.wait_send()

    @pl.when(first)
    def _():
        keep_dx.start()
        keep_dx.wait()
        down.wait_recv()
        c_cur[...] = z_in[...]

    save_dh(1, lax.rem(layers, 2)).wait()
    save_dh(0, lax.rem(layers + 1, 2)).wait()

    def grad_step(i, carry):
        layer, slot = layers - 1 - i, lax.rem(i, 2)
        for copy in load_rest(layer, slot):
            copy.wait()

        @pl.when(first)
        def _():
            for copy in load_second(layer, slot):
                copy.wait()

        @pl.when(i + 1 < layers)
        def _():
            start_grad(i + 1)

        @pl.when(i >= 2)
        def _():
            swap(i - 2).wait_send()

        x0 = xb[slot]
        c0 = c_save[layer]
        for f in range(4):
            a = gelu_value(hb[2 + slot, :, cols(f)].astype(F32)).astype(BF16)
            a1b[slot, :, cols(f)] += dot_tn(x0, dhb[2 + slot, :, cols(f)])
            a2b[slot, cols(f), :] += dot_tn(a, c0)

        pump(2 * i - 1)

        @pl.when(first)
        def _():
            c = c_cur[...]
            x1 = xb[2 + slot]

            def add(f, a, d):
                a1b[slot, :, cols(f)] += dot_tn(x1, d)
                a2b[slot, cols(f), :] += dot_tn(a.astype(BF16), c)

            c_cur[...] = chain(c, slot, slot, add)

        for f in range(4):
            g1 = a1b[slot, :, cols(f)].astype(BF16)
            g2 = a2b[slot, cols(f), :].astype(BF16)
            own = jnp.where(core == 0, g1, g2)
            other = jnp.where(core == 0, g2, g1)
            for s in range(SUB):
                part[i * SUB + s, f] = own[s * rows:(s + 1) * rows]
                to_sib[slot, s, f] = other[s * rows:(s + 1) * rows]
        swap(i).start()
        pump(2 * i)
        return carry

    lax.fori_loop(0, layers, grad_step, 0)

    @pl.when(first)
    def _():
        down.start()

    for i in (layers - 2, layers - 1):
        swap(i).wait_send()

    def tail_step(i, carry):
        pump(i)
        return carry

    lax.fori_loop(2 * layers - 1, chunks + 4 * LAG, tail_step, 0)

    @pl.when(first)
    def _():
        down.wait_send()

    @pl.when(pp == 1)
    def _():
        down.wait_recv()
        put = pltpu.make_async_copy(z_in, dx_hbm, s_misc)
        put.start()
        put.wait()

    pltpu.make_async_copy(gi_hbm, gi_hbm, out_local).wait()
    pltpu.make_async_copy(gi_hbm, gi_hbm, out_send).wait()
    pltpu.make_async_copy(go_hbm, go_hbm, out_recv).wait()


def solution(mesh):
    replicas = mesh.shape['dp']

    def device_fn(w_in, w_out, x_saved, h_saved, dy_in, acc_in, acc_out):
        layers, hidden, ff = w_in.shape[1:]
        tokens = dy_in.shape[1]
        blk = ff // 4
        chunks, rows = layers * SUB, blk // SUB
        dma = pltpu.SemaphoreType.DMA
        flops = 2 * tokens * hidden * ff * layers * 8
        call = pl.pallas_call(
            functools.partial(kernel, layers, blk),
            out_shape=(
                jax.ShapeDtypeStruct((layers, hidden, ff), BF16),
                jax.ShapeDtypeStruct((layers, ff, hidden), BF16),
                jax.ShapeDtypeStruct((tokens, hidden), BF16),
                jax.ShapeDtypeStruct((layers, tokens, ff), BF16),
            ),
            in_specs=[pl.BlockSpec(memory_space=pl.ANY)] * 7,
            out_specs=[pl.BlockSpec(memory_space=pl.ANY)] * 4,
            scratch_shapes=[
                pltpu.VMEM((chunks, 4, rows, hidden), BF16),
                pltpu.VMEM((chunks, 4, rows, hidden), BF16),
                pltpu.VMEM((chunks, 2, rows, hidden), BF16),
                pltpu.VMEM((chunks, rows, hidden), BF16),
                pltpu.VMEM((chunks, 4, rows, hidden), BF16),
                pltpu.VMEM((2, SUB, 4, rows, hidden), BF16),
                pltpu.VMEM((2, hidden, ff), BF16),
                pltpu.VMEM((2, ff, hidden), BF16),
                pltpu.VMEM((4, tokens, ff), BF16),
                pltpu.VMEM((4, tokens, hidden), BF16),
                pltpu.VMEM((4, tokens, ff), BF16),
                pltpu.VMEM((2, hidden, ff), F32),
                pltpu.VMEM((2, ff, hidden), F32),
                pltpu.VMEM((layers, tokens, hidden), BF16),
                pltpu.VMEM((tokens, hidden), BF16),
                pltpu.VMEM((8, 128), F32),
                pltpu.VMEM((tokens, hidden), BF16),
                dma((2,)), dma((2,)), dma((4,)), dma((4,)), dma((2,)), dma((2,)), dma((2,)), dma((2,)), dma,
                dma((2,)), dma((layers,)),
                dma((chunks,)), dma((chunks,)), dma((chunks,)), dma((chunks,)),
                dma((chunks,)), dma((chunks,)), dma((chunks,)), dma((chunks,)),
                dma, dma, dma, dma, dma,
            ],
            compiler_params=pltpu.CompilerParams(collective_id=0, has_side_effects=True, vmem_limit_bytes=67043328),
            cost_estimate=pl.CostEstimate(flops=flops, bytes_accessed=200 << 20, transcendentals=0),
        )
        grad_in, grad_out, dx_out, _ = call(w_in, w_out, x_saved, h_saved, dy_in, acc_in, acc_out)
        scale = 1.0 / replicas
        return (grad_in.astype(F32) * scale)[None], (grad_out.astype(F32) * scale)[None], dx_out[None]

    return jax.shard_map(device_fn, mesh=mesh, in_specs=(P('pp'), P('pp'), P('pp', None, None, 'dp'), P('pp', None, None, 'dp'), P('pp', 'dp'), P('pp', 'dp'), P('pp', 'dp')), out_specs=(P('pp'), P('pp'), P('pp', 'dp')), check_vma=False)
```

time: 668 us -> 218 us (0.33); the launches traced: 658 us -> 217 us
  matrix products: 257 us -> 0 us
  waiting for transfers between devices: 218 us -> 0 us
  Pallas kernels: 0 us -> 193 us
  local copies, waits for them, and re-layouts: 138 us -> 0.71 us
  between operations: 16 us -> 0.64 us
    dot_general x128 -> x0, matrix products: 257 us -> none  [the longest x32 95.5 us: layer_backward(): lax.dot_general(act_bf, cot_in, (((0,), (0,)), ((), ())), preferred_eleme...]
    psum x1 -> x0, waiting for transfers between devices: 208 us -> none  [device_fn(): sum_first = lax.psum(jnp.stack(final_state[1]).astype(jnp.bfloat16), 'dp')]
    pallas_call x0 -> x1, Pallas kernels: none -> 193 us  [device_fn(): call(w_in, w_out, x_saved, h_saved, dy_in, acc_in, acc_out)]
    unnamed x88 -> x3, local copies, waits for them, and re-layouts: 63.9 us -> 0.71 us
    cond x337 -> x0, local copies, waits for them, and re-layouts: 50 us -> none
    squeeze x1 -> x0, local copies, waits for them, and re-layouts: 12.6 us -> none  [device_fn(): acc_second = [acc_out[0, 0, layer_id] for layer_id in range(layers)]]
    slice x1 -> x0, local copies, waits for them, and re-layouts: 11.1 us -> none  [device_fn(): acc_first = [acc_in[0, 0, layer_id] for layer_id in range(layers)]]
    ppermute x1 -> x0, waiting for transfers between devices: 9.58 us -> none  [loop_body(): cot_next = lax.ppermute(cot_cur, 'pp', perm=down_pairs)]
  transfers between devices with their start and end apart: 3 -> 0, of which waited for: 2 -> 0; matrix products, arithmetic and copies ran while one was open for 4% -> 0% of each run, Pallas kernels for 0% -> 0%
where the time goes in v1:
time: 218 us; the launch traced here: 217 us
  Pallas kernels  193 us (89%)
  other arithmetic  23.2 us (11%)
    pallas_call x1, Pallas kernels, device_fn(): call(w_in, w_out, x_saved, h_saved, dy_in, acc_in, acc_out)  193 us
    broadcast_in_dim x1, other arithmetic, device_fn(): (grad_in.astype(F32) * scale)[None]  12 us
    broadcast_in_dim x1, other arithmetic, device_fn(): (grad_out.astype(F32) * scale)[None]  11.2 us

profile of v1, /device:TPU:0, one launch (start us, length us, event | category | flops | bytes accessed | tf_op | source)
XLA Modules:
  0.0 217.1 jit_solution(8193593708544636885)
XLA Ops:
  0.6 192.5 %shard_map.94 = (bf16[16,256,1024]{2,1,0:T(8,128)(2,1)}, bf16[16,1024,256]{2,1,0:T(8,128)(2,1)}, bf16[512,256]{1,0:T(8,128)(2,1)}, bf16[16,512,1024]{2,1,0:T(8,128)(2,1)}) custom-call(bf16[1,16,256,1024]{3,2,1,0:T(8,128)(2,1)} %w1_hbm.1, bf16[1,16,1024,256]{3,2,1,0:T(8,128)(2,1)} %w2_hbm.1, bf16[1,2,16,512,256]{4,3,2,1,0:T(8,128)(2,1)} %x_hbm.1, ...), custom_call_target="tpu_custom_call" | custom-call | flops 34359738368 | bytes 209715200 | tf_op jit(solution)/shard_map/pallas_call | solution.py:378
  193.2 12.0 %multiply_bitcast_fusion.1 = f32[1,16,256,1024]{3,2,1,0:T(8,128)} fusion(bf16[16,256,1024]{2,1,0:T(8,128)(2,1)} %get-tuple-element.6), kind=kLoop, calls=%fused_computation.1 | loop fusion | flops 8388608 | bytes 25165824 | tf_op jit(solution)/shard_map/broadcast_in_dim | solution.py:380
  205.1 0.0 copy-start
  205.1 11.2 %multiply_bitcast_fusion = f32[1,16,1024,256]{3,2,1,0:T(8,128)} fusion(bf16[16,1024,256]{2,1,0:T(8,128)(2,1)} %get-tuple-element.7), kind=kLoop, calls=%fused_computation | loop fusion | flops 8388608 | bytes 25165824 | tf_op jit(solution)/shard_map/broadcast_in_dim | solution.py:380
  216.4 0.0 copy-done
  216.4 0.7 copy.11
Async XLA Ops:
  205.1 11.2 %copy-start = (bf16[512,256]{1,0:T(8,128)(2,1)S(1)}, bf16[512,256]{1,0:T(8,128)(2,1)}, u32[]{:S(2)}) copy-start(bf16[512,256]{1,0:T(8,128)(2,1)} %get-tuple-element.8) | copy-start | bytes 786436

commit v2 on v1

--- a/solution.py
+++ b/solution.py
@@ -6,8 +6,9 @@
 from jax.experimental.pallas import tpu as pltpu
 from jax.sharding import PartitionSpec as P
 
-SUB = 4
+SUB = 2
 LAG = 3
+RING = 8
 MESH = pl.DeviceIdType.MESH
 ROOT_2_PI = 0.7978845608028654
 CUBIC = 0.044715
@@ -39,12 +40,12 @@
 
 
 def kernel(layers, blk, w1_hbm, w2_hbm, x_hbm, h_hbm, dy_hbm, acc1_hbm, acc2_hbm,
-           gi_hbm, go_hbm, dx_hbm, dh_hbm,
-           part, from_sib, rs1_in, rs2_in, full, to_sib,
-           w1b, w2b, hb, xb, dhb, a1b, a2b, c_save, c_cur, c_sum, z_in,
+           full, other, dx, dh_hbm,
+           part, from_sib, rs1_in, rs2_in, to_sib,
+           w1b, w2b, hb, xb, dhb, a1b, a2b, c_save, c_cur, z_in,
            sw1, sw2, sh, sx, sdh_in, sdh_out, sa1, sa2, s_misc,
            sib_send, sib_recv, rs1_send, rs1_recv, rs2_send, rs2_recv,
-           ag2_send, ag2_recv, ag1_send, ag1_recv, out_local, out_send, out_recv,
+           ag2_send, ag2_recv, ag1_send, ag1_recv, out_send, out_recv,
            z_send, z_recv):
     pp = lax.axis_index('pp')
     dp = lax.axis_index('dp')
@@ -102,20 +103,20 @@
 
     def rs1(k):
         half = 2 * (1 - b1)
-        return pltpu.make_async_remote_copy(part.at[k, pl.ds(half, 2)], rs1_in.at[k], rs1_send.at[k], rs1_recv.at[k],
+        return pltpu.make_async_remote_copy(part.at[k, pl.ds(half, 2)], rs1_in.at[k], rs1_send.at[lax.rem(k, RING)], rs1_recv.at[lax.rem(k, RING)],
                                             device_id=(pp, n1), device_id_type=MESH)
 
     def rs2(k):
-        return pltpu.make_async_remote_copy(part.at[k, 2 * b1 + 1 - b2], rs2_in.at[k], rs2_send.at[k], rs2_recv.at[k],
+        return pltpu.make_async_remote_copy(part.at[k, 2 * b1 + 1 - b2], rs2_in.at[k], rs2_send.at[lax.rem(k, RING)], rs2_recv.at[lax.rem(k, RING)],
                                             device_id=(pp, n2), device_id_type=MESH)
 
     def ag2(k):
-        return pltpu.make_async_remote_copy(full.at[k, quarter], full.at[k, quarter], ag2_send.at[k], ag2_recv.at[k],
+        return pltpu.make_async_remote_copy(full.at[k, quarter], full.at[k, quarter], ag2_send.at[lax.rem(k, RING)], ag2_recv.at[lax.rem(k, RING)],
                                             device_id=(pp, n2), device_id_type=MESH)
 
     def ag1(k):
         mine = full.at[k, pl.ds(2 * b1, 2)]
-        return pltpu.make_async_remote_copy(mine, mine, ag1_send.at[k], ag1_recv.at[k],
+        return pltpu.make_async_remote_copy(mine, mine, ag1_send.at[lax.rem(k, RING)], ag1_recv.at[lax.rem(k, RING)],
                                             device_id=(pp, n1), device_id_type=MESH)
 
     def swap(step):
@@ -125,22 +126,8 @@
                                             device_id=(pp, sib), device_id_type=MESH)
 
     def emit(k):
-        layer = layers - 1 - lax.div(k, SUB)
-        row = pl.multiple_of(lax.rem(k, SUB) * rows, rows)
-
-        def send(src, dst):
-            pltpu.make_async_copy(src, dst, out_local).start()
-            pltpu.make_async_remote_copy(src, dst, out_send, out_recv, device_id=(pp, sib), device_id_type=MESH).start()
-
-        @pl.when(core == 0)
-        def _():
-            for q in range(4):
-                send(full.at[k, q], gi_hbm.at[layer, pl.ds(row, rows), pl.ds(q * blk, blk)])
-
-        @pl.when(core == 1)
-        def _():
-            for q in range(4):
-                send(full.at[k, q], go_hbm.at[layer, pl.ds(q * blk + row, rows), :])
+        pltpu.make_async_remote_copy(full.at[k], other.at[k], out_send, out_recv,
+                                     device_id=(pp, sib), device_id_type=MESH).start()
 
     def pump(i):
         def phase(n, body):
@@ -230,7 +217,6 @@
     lax.fori_loop(0, layers, chain_step, 0)
 
     down = pltpu.make_async_remote_copy(c_cur, z_in, z_send, z_recv, device_id=(1 - pp, dp), device_id_type=MESH)
-    keep_dx = pltpu.make_async_copy(c_cur, dx_hbm, s_misc)
 
     @pl.when(pp == 1)
     def _():
@@ -239,10 +225,7 @@
 
     @pl.when(first)
     def _():
-        keep_dx.start()
-        keep_dx.wait()
-        down.wait_recv()
-        c_cur[...] = z_in[...]
+        dx[...] = c_cur[...]
 
     save_dh(1, lax.rem(layers, 2)).wait()
     save_dh(0, lax.rem(layers + 1, 2)).wait()
@@ -276,6 +259,11 @@
 
         @pl.when(first)
         def _():
+            @pl.when(i == 0)
+            def _():
+                down.wait_recv()
+                c_cur[...] = z_in[...]
+
             c = c_cur[...]
             x1 = xb[2 + slot]
 
@@ -319,13 +307,46 @@
     @pl.when(pp == 1)
     def _():
         down.wait_recv()
-        put = pltpu.make_async_copy(z_in, dx_hbm, s_misc)
-        put.start()
-        put.wait()
-
-    pltpu.make_async_copy(gi_hbm, gi_hbm, out_local).wait()
-    pltpu.make_async_copy(gi_hbm, gi_hbm, out_send).wait()
-    pltpu.make_async_copy(go_hbm, go_hbm, out_recv).wait()
+        dx[...] = z_in[...]
+
+    pltpu.make_async_copy(full, full, out_send).wait()
+    pltpu.make_async_copy(other, other, out_recv).wait()
+
+
+def widen(layers, blk, scale, own, other, dx, gi_hbm, go_hbm, dx_hbm, gi_buf, go_buf, gi_sem, go_sem, dx_sem):
+    put_dx = pltpu.make_async_copy(dx, dx_hbm, dx_sem)
+    put_dx.start()
+    core = lax.rem(lax.axis_index('dp'), 2)
+    rows = blk // SUB
+
+    def step(i, carry):
+        layer, slot = layers - 1 - i, lax.rem(i, 2)
+        puts = (pltpu.make_async_copy(gi_buf.at[slot], gi_hbm.at[layer], gi_sem.at[slot]),
+                pltpu.make_async_copy(go_buf.at[slot], go_hbm.at[layer], go_sem.at[slot]))
+
+        @pl.when(i >= 2)
+        def _():
+            for put in puts:
+                put.wait()
+
+        def fill(gi, go):
+            for q in range(4):
+                for s in range(SUB):
+                    r = slice(s * rows, (s + 1) * rows)
+                    gi_buf[slot, r, q * blk:(q + 1) * blk] = gi[i * SUB + s, q].astype(F32) * scale
+                    go_buf[slot, q * blk + s * rows:q * blk + (s + 1) * rows, :] = go[i * SUB + s, q].astype(F32) * scale
+
+        pl.when(core == 0)(lambda: fill(own, other))
+        pl.when(core == 1)(lambda: fill(other, own))
+        for put in puts:
+            put.start()
+        return carry
+
+    lax.fori_loop(0, layers, step, 0)
+    for slot in range(2):
+        pltpu.make_async_copy(gi_buf.at[slot], gi_hbm.at[slot], gi_sem.at[slot]).wait()
+        pltpu.make_async_copy(go_buf.at[slot], go_hbm.at[slot], go_sem.at[slot]).wait()
+    put_dx.wait()
 
 
 def solution(mesh):
@@ -341,19 +362,18 @@
         call = pl.pallas_call(
             functools.partial(kernel, layers, blk),
             out_shape=(
-                jax.ShapeDtypeStruct((layers, hidden, ff), BF16),
-                jax.ShapeDtypeStruct((layers, ff, hidden), BF16),
-                jax.ShapeDtypeStruct((tokens, hidden), BF16),
+                pltpu.VMEM((chunks, 4, rows, hidden), BF16),
+                pltpu.VMEM((chunks, 4, rows, hidden), BF16),
+                pltpu.VMEM((tokens, hidden), BF16),
                 jax.ShapeDtypeStruct((layers, tokens, ff), BF16),
             ),
             in_specs=[pl.BlockSpec(memory_space=pl.ANY)] * 7,
-            out_specs=[pl.BlockSpec(memory_space=pl.ANY)] * 4,
+            out_specs=[pl.BlockSpec(memory_space=pltpu.VMEM)] * 3 + [pl.BlockSpec(memory_space=pl.ANY)],
             scratch_shapes=[
                 pltpu.VMEM((chunks, 4, rows, hidden), BF16),
                 pltpu.VMEM((chunks, 4, rows, hidden), BF16),
                 pltpu.VMEM((chunks, 2, rows, hidden), BF16),
                 pltpu.VMEM((chunks, rows, hidden), BF16),
-                pltpu.VMEM((chunks, 4, rows, hidden), BF16),
                 pltpu.VMEM((2, SUB, 4, rows, hidden), BF16),
                 pltpu.VMEM((2, hidden, ff), BF16),
                 pltpu.VMEM((2, ff, hidden), BF16),
@@ -364,19 +384,26 @@
                 pltpu.VMEM((2, ff, hidden), F32),
                 pltpu.VMEM((layers, tokens, hidden), BF16),
                 pltpu.VMEM((tokens, hidden), BF16),
-                pltpu.VMEM((8, 128), F32),
                 pltpu.VMEM((tokens, hidden), BF16),
                 dma((2,)), dma((2,)), dma((4,)), dma((4,)), dma((2,)), dma((2,)), dma((2,)), dma((2,)), dma,
                 dma((2,)), dma((layers,)),
-                dma((chunks,)), dma((chunks,)), dma((chunks,)), dma((chunks,)),
-                dma((chunks,)), dma((chunks,)), dma((chunks,)), dma((chunks,)),
-                dma, dma, dma, dma, dma,
+                dma((RING,)), dma((RING,)), dma((RING,)), dma((RING,)),
+                dma((RING,)), dma((RING,)), dma((RING,)), dma((RING,)),
+                dma, dma, dma, dma,
             ],
-            compiler_params=pltpu.CompilerParams(collective_id=0, has_side_effects=True, vmem_limit_bytes=67043328),
+            compiler_params=pltpu.CompilerParams(collective_id=0, has_side_effects=True, vmem_limit_bytes=67043328 - (33 << 19)),
             cost_estimate=pl.CostEstimate(flops=flops, bytes_accessed=200 << 20, transcendentals=0),
         )
-        grad_in, grad_out, dx_out, _ = call(w_in, w_out, x_saved, h_saved, dy_in, acc_in, acc_out)
-        scale = 1.0 / replicas
-        return (grad_in.astype(F32) * scale)[None], (grad_out.astype(F32) * scale)[None], dx_out[None]
+        own, other, dx, _ = call(w_in, w_out, x_saved, h_saved, dy_in, acc_in, acc_out)
+        grad_in, grad_out, dx_out = pl.pallas_call(
+            functools.partial(widen, layers, blk, 1.0 / replicas),
+            out_shape=(jax.ShapeDtypeStruct((layers, hidden, ff), F32), jax.ShapeDtypeStruct((layers, ff, hidden), F32),
+                       jax.ShapeDtypeStruct((tokens, hidden), BF16)),
+            in_specs=[pl.BlockSpec(memory_space=pltpu.VMEM)] * 3,
+            out_specs=[pl.BlockSpec(memory_space=pl.ANY)] * 3,
+            scratch_shapes=[pltpu.VMEM((2, hidden, ff), F32), pltpu.VMEM((2, ff, hidden), F32), dma((2,)), dma((2,)), dma],
+            compiler_params=pltpu.CompilerParams(vmem_limit_bytes=12 << 20),
+        )(own, other, dx)
+        return grad_in[None], grad_out[None], dx_out[None]
 
     return jax.shard_map(device_fn, mesh=mesh, in_specs=(P('pp'), P('pp'), P('pp', None, None, 'dp'), P('pp', None, None, 'dp'), P('pp', 'dp'), P('pp', 'dp'), P('pp', 'dp')), out_specs=(P('pp'), P('pp'), P('pp', 'dp')), check_vma=False)

time: 218 us -> 199 us (0.913)
  other arithmetic: 23.2 us -> 0 us
  Pallas kernels: 193 us -> 197 us
    broadcast_in_dim x2 -> x0, other arithmetic: 23.2 us -> none  [the longest x1 12 us: device_fn(): (grad_in.astype(F32) * scale)[None]]
    pallas_call x0 -> x1, Pallas kernels: none -> 12.2 us  [device_fn(): pl.pallas_call(functools.partial(widen, layers, blk, 1.0 / replicas), out...]
    pallas_call x1, Pallas kernels: 193 us -> 185 us  [device_fn(): call(w_in, w_out, x_saved, h_saved, dy_in, acc_in, acc_out)]
where the time goes in v2:
time: 199 us; the launch traced here: 198 us
  Pallas kernels  197 us (99%)
    pallas_call x1, Pallas kernels, device_fn(): call(w_in, w_out, x_saved, h_saved, dy_in, acc_in, acc_out)  185 us
    pallas_call x1, Pallas kernels, device_fn(): pl.pallas_call(functools.partial(widen, layers, blk, 1.0 / replicas), out...  12.2 us

profile of v2, /device:TPU:0, one launch (start us, length us, event | category | flops | bytes accessed | tf_op | source)
XLA Modules:
  0.0 197.8 jit_solution(15949481221976031083)
XLA Ops:
  0.6 185.0 %shard_map.94 = (bf16[32,4,128,256]{3,2,1,0:T(8,128)(2,1)S(1)}, bf16[32,4,128,256]{3,2,1,0:T(8,128)(2,1)S(1)}, bf16[512,256]{1,0:T(8,128)(2,1)S(1)}, bf16[16,512,1024]{2,1,0:T(8,128)(2,1)}) custom-call(bf16[1,16,256,1024]{3,2,1,0:T(8,128)(2,1)} %w1_hbm.1, bf16[1,16,1024,256]{3,2,1,0:T(8,128)(2,1)} %w2_hbm.1, bf16[1,2,16,512,256]{4,3,2,1,0:T(8,128)(2,1)} %x_hbm.1, ...), custom_call_target="tpu_custom_call" | custom-call | flops 34359738368 | bytes 209715200 | tf_op jit(solution)/shard_map/pallas_call | solution.py:397
  185.7 12.2 %shard_map.95 = (f32[16,256,1024]{2,1,0:T(8,128)}, f32[16,1024,256]{2,1,0:T(8,128)}, bf16[512,256]{1,0:T(8,128)(2,1)}) custom-call(bf16[32,4,128,256]{3,2,1,0:T(8,128)(2,1)S(1)} %get-tuple-element.9.own, bf16[32,4,128,256]{3,2,1,0:T(8,128)(2,1)S(1)} %get-tuple-element.10.other, bf16[512,256]{1,0:T(8,128)(2,1)S(1)} %get-tuple-element.11.dx), custom_call_target="tpu_custom_call" | custom-call | tf_op jit(solution)/shard_map/pallas_call | solution.py:398

commit v3 on v2

--- a/solution.py
+++ b/solution.py
@@ -9,6 +9,12 @@
 SUB = 2
 LAG = 3
 RING = 8
+DEPTH = 4
+EARLY = 3
+GAP = 5
+LENDS = (4, 8)
+LENT = len(LENDS)
+TAKE_AT = 12
 MESH = pl.DeviceIdType.MESH
 ROOT_2_PI = 0.7978845608028654
 CUBIC = 0.044715
@@ -39,6 +45,13 @@
     return lax.dot_general(a, b, (((0,), (0,)), ((), ())), preferred_element_type=F32)
 
 
+def layer_of(pp, made, layers):
+    j = made - EARLY
+    late = jnp.minimum(j + 1 + lax.div(j, GAP - 1), layers - 1)
+    early = (made < EARLY).astype(jnp.int32)
+    return layers - 1 - (made + pp * (late + early * (GAP * made - late) - made))
+
+
 def kernel(layers, blk, w1_hbm, w2_hbm, x_hbm, h_hbm, dy_hbm, acc1_hbm, acc2_hbm,
            full, other, dx, dh_hbm,
            part, from_sib, rs1_in, rs2_in, to_sib,
@@ -46,7 +59,8 @@
            sw1, sw2, sh, sx, sdh_in, sdh_out, sa1, sa2, s_misc,
            sib_send, sib_recv, rs1_send, rs1_recv, rs2_send, rs2_recv,
            ag2_send, ag2_recv, ag1_send, ag1_recv, out_send, out_recv,
-           z_send, z_recv):
+           z_send, z_recv,
+           lend_send, lend_recv, back_send, back_recv, sib_free):
     pp = lax.axis_index('pp')
     dp = lax.axis_index('dp')
     core = lax.rem(dp, 2)
@@ -61,13 +75,9 @@
     sib = dp + 1 - 2 * core
     quarter = 2 * b1 + b2
     first = pp == 0
-    chunks = layers * SUB
+    taken = pp * LENT
+    chunks = (layers - LENT + 2 * taken) * SUB
     rows = blk // SUB
-
-    barrier = pltpu.get_barrier_semaphore()
-    for peer in ((pp, sib), (pp, n1), (pp, n2), (1 - pp, dp)):
-        pl.semaphore_signal(barrier, inc=1, device_id=peer, device_id_type=MESH)
-    pl.semaphore_wait(barrier, 4)
 
     def load_w(layer, slot):
         return (pltpu.make_async_copy(w1_hbm.at[0, layer], w1b.at[slot], sw1.at[slot]),
@@ -79,11 +89,15 @@
     def load_x(micro, layer, slot):
         return pltpu.make_async_copy(x_hbm.at[0, micro, layer], xb.at[slot], sx.at[slot])
 
-    def load_rest(layer, slot):
+    def load_sums(layer, slot):
         return (pltpu.make_async_copy(acc1_hbm.at[0, 0, layer], a1b.at[slot], sa1.at[slot]),
                 pltpu.make_async_copy(acc2_hbm.at[0, 0, layer], a2b.at[slot], sa2.at[slot]),
-                pltpu.make_async_copy(dh_hbm.at[layer], dhb.at[2 + slot], sdh_in.at[slot]),
-                load_h(0, layer, 2 + slot), load_x(0, layer, slot))
+                load_x(0, layer, slot))
+
+    def load_rest(layer, slot):
+        return load_sums(layer, slot) + (
+            pltpu.make_async_copy(dh_hbm.at[layer], dhb.at[2 + slot], sdh_in.at[slot]),
+            load_h(0, layer, 2 + slot))
 
     def load_second(layer, slot):
         return load_w(layer, slot) + (load_h(1, layer, slot), load_x(1, layer, 2 + slot))
@@ -92,7 +106,7 @@
         return pltpu.make_async_copy(dhb.at[slot], dh_hbm.at[layer], sdh_out.at[slot])
 
     def start_grad(step):
-        layer, slot = layers - 1 - step, lax.rem(step, 2)
+        layer, slot = layer_of(pp, step + EARLY * pp, layers), lax.rem(step, 2)
         for copy in load_rest(layer, slot):
             copy.start()
 
@@ -101,53 +115,106 @@
             for copy in load_second(layer, slot):
                 copy.start()
 
+    def place(k):
+        p, sub = lax.div(k, SUB), lax.rem(k, SUB)
+        late = sum((p >= m - n).astype(jnp.int32) for n, m in enumerate(LENDS))
+        after = (p >= TAKE_AT).astype(jnp.int32)
+        past = (p >= TAKE_AT + LENT).astype(jnp.int32)
+        zero = p + late
+        one = p + (layers - TAKE_AT) * (after - past) - LENT * past
+        return (zero + pp * (one - zero)) * SUB + sub
+
+    def remote(src, dst, send, recv, peer):
+        return pltpu.make_async_remote_copy(src, dst, send, recv, device_id=peer, device_id_type=MESH)
+
     def rs1(k):
-        half = 2 * (1 - b1)
-        return pltpu.make_async_remote_copy(part.at[k, pl.ds(half, 2)], rs1_in.at[k], rs1_send.at[lax.rem(k, RING)], rs1_recv.at[lax.rem(k, RING)],
-                                            device_id=(pp, n1), device_id_type=MESH)
+        b, r = place(k), lax.rem(k, RING)
+        return remote(part.at[b, pl.ds(2 * (1 - b1), 2)], rs1_in.at[b], rs1_send.at[r], rs1_recv.at[r], (pp, n1))
 
     def rs2(k):
-        return pltpu.make_async_remote_copy(part.at[k, 2 * b1 + 1 - b2], rs2_in.at[k], rs2_send.at[lax.rem(k, RING)], rs2_recv.at[lax.rem(k, RING)],
-                                            device_id=(pp, n2), device_id_type=MESH)
+        b, r = place(k), lax.rem(k, RING)
+        return remote(part.at[b, 2 * b1 + 1 - b2], rs2_in.at[b], rs2_send.at[r], rs2_recv.at[r], (pp, n2))
 
     def ag2(k):
-        return pltpu.make_async_remote_copy(full.at[k, quarter], full.at[k, quarter], ag2_send.at[lax.rem(k, RING)], ag2_recv.at[lax.rem(k, RING)],
-                                            device_id=(pp, n2), device_id_type=MESH)
+        b, r = place(k), lax.rem(k, RING)
+        return remote(full.at[b, quarter], full.at[b, quarter], ag2_send.at[r], ag2_recv.at[r], (pp, n2))
 
     def ag1(k):
-        mine = full.at[k, pl.ds(2 * b1, 2)]
-        return pltpu.make_async_remote_copy(mine, mine, ag1_send.at[lax.rem(k, RING)], ag1_recv.at[lax.rem(k, RING)],
-                                            device_id=(pp, n1), device_id_type=MESH)
-
-    def swap(step):
-        slot = lax.rem(step, 2)
-        return pltpu.make_async_remote_copy(to_sib.at[slot], from_sib.at[pl.ds(step * SUB, SUB)],
-                                            sib_send.at[slot], sib_recv.at[step],
-                                            device_id=(pp, sib), device_id_type=MESH)
-
-    def emit(k):
-        pltpu.make_async_remote_copy(full.at[k], other.at[k], out_send, out_recv,
-                                     device_id=(pp, sib), device_id_type=MESH).start()
+        b, r = place(k), lax.rem(k, RING)
+        mine = full.at[b, pl.ds(2 * b1, 2)]
+        return remote(mine, mine, ag1_send.at[r], ag1_recv.at[r], (pp, n1))
+
+    def swap(made):
+        slot, held = lax.rem(made, 2), lax.rem(made, DEPTH)
+        return remote(to_sib.at[slot], from_sib.at[held], sib_send.at[slot], sib_recv.at[held], (pp, sib))
+
+    def freed(made):
+        @pl.when(made + DEPTH < layers)
+        def _():
+            pl.semaphore_signal(sib_free, inc=1, device_id=(pp, sib), device_id_type=MESH)
+
+    def lend(n):
+        return remote(part.at[pl.ds(LENDS[n] * SUB, SUB)], part.at[pl.ds((layers + n) * SUB, SUB)],
+                      lend_send.at[n], lend_recv.at[n], (1 - pp, dp))
+
+    def give_back(n):
+        return remote(full.at[layers * SUB + n], full.at[LENDS[n // SUB] * SUB + n % SUB],
+                      back_send.at[n], back_recv.at[n], (1 - pp, dp))
+
+    def emit(b):
+        remote(full.at[b], other.at[b], out_send, out_recv, (pp, sib)).start()
+
+    def lend_out(n):
+        made = LENDS[n]
+        swap(made).wait_recv()
+        for t in range(SUB):
+            part[made * SUB + t] = part[made * SUB + t] + from_sib[made % DEPTH, t]
+        freed(made)
+        lend(n).start()
+
+    def chunk_at(step):
+        turn, at = lax.div(step, GAP), lax.rem(step, GAP)
+        chain = (step < layers).astype(jnp.int32)
+        one = (1 - chain) * (step - layers + EARLY * SUB) + chain * (2 * turn + lax.div(at, 2))
+        k = step + pp * (one - step)
+        idle = (pp == 1) & (step < layers) & ((turn >= EARLY) | ((at != 1) & (at != 3)))
+        return k, (step >= 0) & (k < chunks) & jnp.logical_not(idle)
 
     def pump(i):
         def phase(n, body):
-            k = i - n * LAG
-            pl.when((k >= 0) & (k < chunks))(lambda: body(k))
+            k, there = chunk_at(i - n * LAG)
+            pl.when(there)(lambda: body(k))
 
         def sum0(k):
-            @pl.when(lax.rem(k, SUB) == 0)
+            b, sub = place(k), lax.rem(k, SUB)
+            made = lax.div(b, SUB)
+
+            @pl.when(made < layers)
             def _():
-                swap(lax.div(k, SUB)).wait_recv()
-            part[k] = part[k] + from_sib[k]
+                @pl.when(sub == 0)
+                def _():
+                    swap(made).wait_recv()
+                part[b] = part[b] + from_sib[lax.rem(made, DEPTH), sub]
+
+                @pl.when(sub == SUB - 1)
+                def _():
+                    freed(made)
+
+            for n in range(LENT):
+                @pl.when((made == layers + n) & (sub == 0))
+                def _():
+                    lend(n).wait_recv()
 
         def sum1(k):
             rs1(k).wait()
+            b = place(k)
             for j in range(2):
-                part[k, 2 * b1 + j] = part[k, 2 * b1 + j] + rs1_in[k, j]
+                part[b, 2 * b1 + j] = part[b, 2 * b1 + j] + rs1_in[b, j]
 
         def sum2(k):
             rs2(k).wait()
-            full[k, quarter] = part[k, quarter] + rs2_in[k]
+            b = place(k)
+            full[b, quarter] = part[b, quarter] + rs2_in[b]
 
         def done2(k):
             ag2(k).wait()
@@ -155,7 +222,10 @@
 
         def done1(k):
             ag1(k).wait()
-            emit(k)
+            b = place(k)
+            pl.when(b < layers * SUB)(lambda: emit(b))
+            for n in range(LENT * SUB):
+                pl.when(b == layers * SUB + n)(lambda n=n: give_back(n).start())
 
         phase(2, sum2)
         phase(1, sum1)
@@ -173,6 +243,15 @@
     first_c.start()
     for copy in load_w(layers - 1, 0) + (load_h(0, layers - 1, 0),):
         copy.start()
+    @pl.when(pp == 1)
+    def _():
+        for copy in load_sums(layers - 1, 0):
+            copy.start()
+
+    barrier = pltpu.get_barrier_semaphore()
+    for peer in ((pp, sib), (pp, n1), (pp, n2), (1 - pp, dp)):
+        pl.semaphore_signal(barrier, inc=1, device_id=peer, device_id_type=MESH)
+    pl.semaphore_wait(barrier, 4)
     first_c.wait()
 
     def chain(c, hs, ws, with_grads):
@@ -186,6 +265,33 @@
             total = back if total is None else total + back
         return (c.astype(F32) + total).astype(BF16)
 
+    def first_grads(layer, slot, hs, ds):
+        x0 = xb[slot]
+        c0 = c_save[layer]
+        for f in range(4):
+            a = gelu_value(hb[hs, :, cols(f)].astype(F32)).astype(BF16)
+            a1b[slot, :, cols(f)] += dot_tn(x0, dhb[ds, :, cols(f)])
+            a2b[slot, cols(f), :] += dot_tn(a, c0)
+
+    def publish(made, slot):
+        @pl.when(made >= 2)
+        def _():
+            swap(made - 2).wait_send()
+
+        for f in range(4):
+            g1 = a1b[slot, :, cols(f)].astype(BF16)
+            g2 = a2b[slot, cols(f), :].astype(BF16)
+            own = jnp.where(core == 0, g1, g2)
+            rest = jnp.where(core == 0, g2, g1)
+            for t in range(SUB):
+                part[made * SUB + t, f] = own[t * rows:(t + 1) * rows]
+                to_sib[lax.rem(made, 2), t, f] = rest[t * rows:(t + 1) * rows]
+
+        @pl.when(made >= DEPTH)
+        def _():
+            pl.semaphore_wait(sib_free, 1)
+        swap(made).start()
+
     def chain_step(i, carry):
         layer, slot = layers - 1 - i, lax.rem(i, 2)
         for copy in load_w(layer, slot) + (load_h(0, layer, slot),):
@@ -212,6 +318,26 @@
 
         c_cur[...] = chain(c, slot, slot, keep)
         save_dh(layer, slot).start()
+
+        turn, at = lax.div(i, GAP), lax.rem(i, GAP)
+
+        @pl.when((pp == 1) & (at == 0) & (turn < EARLY))
+        def _():
+            held = lax.rem(turn, 2)
+            for copy in load_sums(layer, held):
+                copy.wait()
+
+            @pl.when(turn + 1 < EARLY)
+            def _():
+                for copy in load_sums(layer - GAP, 1 - held):
+                    copy.start()
+
+            first_grads(layer, held, slot, slot)
+            publish(turn, held)
+
+        @pl.when(pp == 1)
+        def _():
+            pump(i)
         return carry
 
     lax.fori_loop(0, layers, chain_step, 0)
@@ -221,7 +347,6 @@
     @pl.when(pp == 1)
     def _():
         down.start()
-        down.wait_send()
 
     @pl.when(first)
     def _():
@@ -231,7 +356,8 @@
     save_dh(0, lax.rem(layers + 1, 2)).wait()
 
     def grad_step(i, carry):
-        layer, slot = layers - 1 - i, lax.rem(i, 2)
+        made = i + EARLY * pp
+        layer, slot = layer_of(pp, made, layers), lax.rem(i, 2)
         for copy in load_rest(layer, slot):
             copy.wait()
 
@@ -240,22 +366,22 @@
             for copy in load_second(layer, slot):
                 copy.wait()
 
-        @pl.when(i + 1 < layers)
+        @pl.when(made + 1 < layers)
         def _():
             start_grad(i + 1)
 
-        @pl.when(i >= 2)
-        def _():
-            swap(i - 2).wait_send()
-
-        x0 = xb[slot]
-        c0 = c_save[layer]
-        for f in range(4):
-            a = gelu_value(hb[2 + slot, :, cols(f)].astype(F32)).astype(BF16)
-            a1b[slot, :, cols(f)] += dot_tn(x0, dhb[2 + slot, :, cols(f)])
-            a2b[slot, cols(f), :] += dot_tn(a, c0)
-
-        pump(2 * i - 1)
+        first_grads(layer, slot, 2 + slot, 2 + slot)
+
+        lent = sum((made > m).astype(jnp.int32) for m in LENDS)
+        step = 2 * (made - lent - 1) + pp * (layers + 2 * (lent - EARLY))
+        still = functools.reduce(jnp.logical_or, [first & (made == m + 1) for m in LENDS], i == 0)
+
+        for n in range(LENT):
+            pl.when(first & (made == LENDS[n] + 1))(functools.partial(lend_out, n))
+
+        @pl.when(jnp.logical_not(still))
+        def _():
+            pump(step)
 
         @pl.when(first)
         def _():
@@ -273,19 +399,14 @@
 
             c_cur[...] = chain(c, slot, slot, add)
 
-        for f in range(4):
-            g1 = a1b[slot, :, cols(f)].astype(BF16)
-            g2 = a2b[slot, cols(f), :].astype(BF16)
-            own = jnp.where(core == 0, g1, g2)
-            other = jnp.where(core == 0, g2, g1)
-            for s in range(SUB):
-                part[i * SUB + s, f] = own[s * rows:(s + 1) * rows]
-                to_sib[slot, s, f] = other[s * rows:(s + 1) * rows]
-        swap(i).start()
-        pump(2 * i)
+        publish(made, slot)
+
+        @pl.when(jnp.logical_not(still))
+        def _():
+            pump(step + 1)
         return carry
 
-    lax.fori_loop(0, layers, grad_step, 0)
+    lax.fori_loop(0, layers - EARLY * pp, grad_step, 0)
 
     @pl.when(first)
     def _():
@@ -298,18 +419,30 @@
         pump(i)
         return carry
 
-    lax.fori_loop(2 * layers - 1, chunks + 4 * LAG, tail_step, 0)
+    ahead = pp * (layers - EARLY * SUB)
+    lax.fori_loop(2 * (layers - LENT - 1) + pp * (layers + 2 * (LENT - EARLY)), chunks + ahead + 4 * LAG, tail_step, 0)
 
     @pl.when(first)
     def _():
-        down.wait_send()
+        for n in range(LENT):
+            lend(n).wait_send()
+        for n in range(LENT * SUB):
+            give_back(n).wait_recv()
+            emit(LENDS[n // SUB] * SUB + n % SUB)
+
+    @pl.when(pp == 1)
+    def _():
+        for n in range(LENT * SUB):
+            give_back(n).wait_send()
+
+    down.wait_send()
 
     @pl.when(pp == 1)
     def _():
         down.wait_recv()
         dx[...] = z_in[...]
 
-    pltpu.make_async_copy(full, full, out_send).wait()
+    pltpu.make_async_copy(other, other, out_send).wait()
     pltpu.make_async_copy(other, other, out_recv).wait()
 
 
@@ -317,10 +450,11 @@
     put_dx = pltpu.make_async_copy(dx, dx_hbm, dx_sem)
     put_dx.start()
     core = lax.rem(lax.axis_index('dp'), 2)
+    pp = lax.axis_index('pp')
     rows = blk // SUB
 
     def step(i, carry):
-        layer, slot = layers - 1 - i, lax.rem(i, 2)
+        layer, slot = layer_of(pp, i, layers), lax.rem(i, 2)
         puts = (pltpu.make_async_copy(gi_buf.at[slot], gi_hbm.at[layer], gi_sem.at[slot]),
                 pltpu.make_async_copy(go_buf.at[slot], go_hbm.at[layer], go_sem.at[slot]))
 
@@ -357,12 +491,13 @@
         tokens = dy_in.shape[1]
         blk = ff // 4
         chunks, rows = layers * SUB, blk // SUB
+        room = chunks + LENT * SUB
         dma = pltpu.SemaphoreType.DMA
         flops = 2 * tokens * hidden * ff * layers * 8
         call = pl.pallas_call(
             functools.partial(kernel, layers, blk),
             out_shape=(
-                pltpu.VMEM((chunks, 4, rows, hidden), BF16),
+                pltpu.VMEM((room, 4, rows, hidden), BF16),
                 pltpu.VMEM((chunks, 4, rows, hidden), BF16),
                 pltpu.VMEM((tokens, hidden), BF16),
                 jax.ShapeDtypeStruct((layers, tokens, ff), BF16),
@@ -370,10 +505,10 @@
             in_specs=[pl.BlockSpec(memory_space=pl.ANY)] * 7,
             out_specs=[pl.BlockSpec(memory_space=pltpu.VMEM)] * 3 + [pl.BlockSpec(memory_space=pl.ANY)],
             scratch_shapes=[
-                pltpu.VMEM((chunks, 4, rows, hidden), BF16),
-                pltpu.VMEM((chunks, 4, rows, hidden), BF16),
-                pltpu.VMEM((chunks, 2, rows, hidden), BF16),
-                pltpu.VMEM((chunks, rows, hidden), BF16),
+                pltpu.VMEM((room, 4, rows, hidden), BF16),
+                pltpu.VMEM((DEPTH, SUB, 4, rows, hidden), BF16),
+                pltpu.VMEM((room, 2, rows, hidden), BF16),
+                pltpu.VMEM((room, rows, hidden), BF16),
                 pltpu.VMEM((2, SUB, 4, rows, hidden), BF16),
                 pltpu.VMEM((2, hidden, ff), BF16),
                 pltpu.VMEM((2, ff, hidden), BF16),
@@ -386,12 +521,13 @@
                 pltpu.VMEM((tokens, hidden), BF16),
                 pltpu.VMEM((tokens, hidden), BF16),
                 dma((2,)), dma((2,)), dma((4,)), dma((4,)), dma((2,)), dma((2,)), dma((2,)), dma((2,)), dma,
-                dma((2,)), dma((layers,)),
+                dma((2,)), dma((DEPTH,)),
                 dma((RING,)), dma((RING,)), dma((RING,)), dma((RING,)),
                 dma((RING,)), dma((RING,)), dma((RING,)), dma((RING,)),
                 dma, dma, dma, dma,
+                dma((LENT,)), dma((LENT,)), dma((LENT * SUB,)), dma((LENT * SUB,)), pltpu.SemaphoreType.REGULAR,
             ],
-            compiler_params=pltpu.CompilerParams(collective_id=0, has_side_effects=True, vmem_limit_bytes=67043328 - (33 << 19)),
+            compiler_params=pltpu.CompilerParams(collective_id=0, has_side_effects=True, vmem_limit_bytes=67043328 - (35 << 19)),
             cost_estimate=pl.CostEstimate(flops=flops, bytes_accessed=200 << 20, transcendentals=0),
         )
         own, other, dx, _ = call(w_in, w_out, x_saved, h_saved, dy_in, acc_in, acc_out)

time: 199 us -> 189 us (0.950)
  Pallas kernels: 197 us -> 187 us
    pallas_call x1, Pallas kernels: 185 us -> 175 us  [device_fn(): call(w_in, w_out, x_saved, h_saved, dy_in, acc_in, acc_out)]
where the time goes in v3:
time: 189 us; the launch traced here: 188 us
  Pallas kernels  187 us (99%)
    pallas_call x1, Pallas kernels, device_fn(): call(w_in, w_out, x_saved, h_saved, dy_in, acc_in, acc_out)  175 us
    pallas_call x1, Pallas kernels, device_fn(): pl.pallas_call(functools.partial(widen, layers, blk, 1.0 / replicas), out...  12.2 us

profile of v3, /device:TPU:0, one launch (start us, length us, event | category | flops | bytes accessed | tf_op | source)
XLA Modules:
  0.0 188.0 jit_solution(11156632188488759287)
XLA Ops:
  0.6 175.1 %shard_map.94 = (bf16[36,4,128,256]{3,2,1,0:T(8,128)(2,1)S(1)}, bf16[32,4,128,256]{3,2,1,0:T(8,128)(2,1)S(1)}, bf16[512,256]{1,0:T(8,128)(2,1)S(1)}, bf16[16,512,1024]{2,1,0:T(8,128)(2,1)}) custom-call(bf16[1,16,256,1024]{3,2,1,0:T(8,128)(2,1)} %w1_hbm.1, bf16[1,16,1024,256]{3,2,1,0:T(8,128)(2,1)} %w2_hbm.1, bf16[1,2,16,512,256]{4,3,2,1,0:T(8,128)(2,1)} %x_hbm.1, ...), custom_call_target="tpu_custom_call" | custom-call | flops 34359738368 | bytes 209715200 | tf_op jit(solution)/shard_map/pallas_call | solution.py:533
  175.8 12.2 %shard_map.95 = (f32[16,256,1024]{2,1,0:T(8,128)}, f32[16,1024,256]{2,1,0:T(8,128)}, bf16[512,256]{1,0:T(8,128)(2,1)}) custom-call(bf16[36,4,128,256]{3,2,1,0:T(8,128)(2,1)S(1)} %get-tuple-element.9.own, bf16[32,4,128,256]{3,2,1,0:T(8,128)(2,1)S(1)} %get-tuple-element.10.other, bf16[512,256]{1,0:T(8,128)(2,1)S(1)} %get-tuple-element.11.dx), custom_call_target="tpu_custom_call" | custom-call | tf_op jit(solution)/shard_map/pallas_call | solution.py:534

commit v4 on v3

--- a/solution.py
+++ b/solution.py
@@ -9,12 +9,14 @@
 SUB = 2
 LAG = 3
 RING = 8
+WIDEN_SLOTS = 4
 DEPTH = 4
-EARLY = 3
-GAP = 5
-LENDS = (4, 8)
-LENT = len(LENDS)
-TAKE_AT = 12
+EARLY = 4
+GAP = 4
+SECOND = 3
+LENDS = {4: (1,), 6: (1,), 8: (1,), 10: (1,)}
+LENT = tuple(m * SUB + t for m, subs in LENDS.items() for t in subs)
+TAKE_AT = 24
 MESH = pl.DeviceIdType.MESH
 ROOT_2_PI = 0.7978845608028654
 CUBIC = 0.044715
@@ -75,8 +77,7 @@
     sib = dp + 1 - 2 * core
     quarter = 2 * b1 + b2
     first = pp == 0
-    taken = pp * LENT
-    chunks = (layers - LENT + 2 * taken) * SUB
+    chunks = layers * SUB - len(LENT) + 2 * len(LENT) * pp
     rows = blk // SUB
 
     def load_w(layer, slot):
@@ -116,13 +117,11 @@
                 copy.start()
 
     def place(k):
-        p, sub = lax.div(k, SUB), lax.rem(k, SUB)
-        late = sum((p >= m - n).astype(jnp.int32) for n, m in enumerate(LENDS))
-        after = (p >= TAKE_AT).astype(jnp.int32)
-        past = (p >= TAKE_AT + LENT).astype(jnp.int32)
-        zero = p + late
-        one = p + (layers - TAKE_AT) * (after - past) - LENT * past
-        return (zero + pp * (one - zero)) * SUB + sub
+        late = sum((k >= c - n).astype(jnp.int32) for n, c in enumerate(LENT))
+        after = (k >= TAKE_AT).astype(jnp.int32)
+        past = (k >= TAKE_AT + len(LENT)).astype(jnp.int32)
+        one = k + (layers * SUB - TAKE_AT) * (after - past) - len(LENT) * past
+        return k + late + pp * (one - k - late)
 
     def remote(src, dst, send, recv, peer):
         return pltpu.make_async_remote_copy(src, dst, send, recv, device_id=peer, device_id_type=MESH)
@@ -154,30 +153,30 @@
             pl.semaphore_signal(sib_free, inc=1, device_id=(pp, sib), device_id_type=MESH)
 
     def lend(n):
-        return remote(part.at[pl.ds(LENDS[n] * SUB, SUB)], part.at[pl.ds((layers + n) * SUB, SUB)],
-                      lend_send.at[n], lend_recv.at[n], (1 - pp, dp))
+        return remote(part.at[LENT[n]], part.at[layers * SUB + n], lend_send.at[n], lend_recv.at[n], (1 - pp, dp))
 
     def give_back(n):
-        return remote(full.at[layers * SUB + n], full.at[LENDS[n // SUB] * SUB + n % SUB],
-                      back_send.at[n], back_recv.at[n], (1 - pp, dp))
+        return remote(full.at[layers * SUB + n], full.at[LENT[n]], back_send.at[n], back_recv.at[n], (1 - pp, dp))
 
     def emit(b):
         remote(full.at[b], other.at[b], out_send, out_recv, (pp, sib)).start()
 
-    def lend_out(n):
-        made = LENDS[n]
-        swap(made).wait_recv()
-        for t in range(SUB):
-            part[made * SUB + t] = part[made * SUB + t] + from_sib[made % DEPTH, t]
+    def lend_out(made):
+        if 0 in LENDS[made]:
+            swap(made).wait_recv()
+        for t in LENDS[made]:
+            c = made * SUB + t
+            part[c] = part[c] + from_sib[made % DEPTH, t]
         freed(made)
-        lend(n).start()
+        for t in LENDS[made]:
+            lend(LENT.index(made * SUB + t)).start()
 
     def chunk_at(step):
         turn, at = lax.div(step, GAP), lax.rem(step, GAP)
-        chain = (step < layers).astype(jnp.int32)
-        one = (1 - chain) * (step - layers + EARLY * SUB) + chain * (2 * turn + lax.div(at, 2))
+        chain = (step < layers + SUB).astype(jnp.int32)
+        one = (1 - chain) * (step - layers - SUB + EARLY * SUB) + chain * (2 * turn + (at == SECOND).astype(jnp.int32))
         k = step + pp * (one - step)
-        idle = (pp == 1) & (step < layers) & ((turn >= EARLY) | ((at != 1) & (at != 3)))
+        idle = (pp == 1) & (chain == 1) & ((turn >= EARLY) | ((at != 1) & (at != SECOND)))
         return k, (step >= 0) & (k < chunks) & jnp.logical_not(idle)
 
     def pump(i):
@@ -186,8 +185,8 @@
             pl.when(there)(lambda: body(k))
 
         def sum0(k):
-            b, sub = place(k), lax.rem(k, SUB)
-            made = lax.div(b, SUB)
+            b = place(k)
+            made, sub = lax.div(b, SUB), lax.rem(b, SUB)
 
             @pl.when(made < layers)
             def _():
@@ -200,10 +199,8 @@
                 def _():
                     freed(made)
 
-            for n in range(LENT):
-                @pl.when((made == layers + n) & (sub == 0))
-                def _():
-                    lend(n).wait_recv()
+            for n in range(len(LENT)):
+                pl.when(b == layers * SUB + n)(lambda n=n: lend(n).wait_recv())
 
         def sum1(k):
             rs1(k).wait()
@@ -224,7 +221,7 @@
             ag1(k).wait()
             b = place(k)
             pl.when(b < layers * SUB)(lambda: emit(b))
-            for n in range(LENT * SUB):
+            for n in range(len(LENT)):
                 pl.when(b == layers * SUB + n)(lambda n=n: give_back(n).start())
 
         phase(2, sum2)
@@ -335,7 +332,7 @@
             first_grads(layer, held, slot, slot)
             publish(turn, held)
 
-        @pl.when(pp == 1)
+        @pl.when((pp == 1) & (i > 0))
         def _():
             pump(i)
         return carry
@@ -372,16 +369,18 @@
 
         first_grads(layer, slot, 2 + slot, 2 + slot)
 
-        lent = sum((made > m).astype(jnp.int32) for m in LENDS)
-        step = 2 * (made - lent - 1) + pp * (layers + 2 * (lent - EARLY))
-        still = functools.reduce(jnp.logical_or, [first & (made == m + 1) for m in LENDS], i == 0)
-
-        for n in range(LENT):
-            pl.when(first & (made == LENDS[n] + 1))(functools.partial(lend_out, n))
-
-        @pl.when(jnp.logical_not(still))
+        def ready(m):
+            return m * SUB - (1 - pp) * sum((m * SUB > c).astype(jnp.int32) for c in LENT)
+
+        step = ready(made - 1) + pp * (layers + SUB - EARLY * SUB)
+        count = jnp.where(made == 0, 0, ready(made) - ready(made - 1))
+
+        @pl.when(count > 0)
         def _():
             pump(step)
+
+        for m in LENDS:
+            pl.when(first & (made == m + 1))(functools.partial(lend_out, m))
 
         @pl.when(first)
         def _():
@@ -401,7 +400,7 @@
 
         publish(made, slot)
 
-        @pl.when(jnp.logical_not(still))
+        @pl.when(count > 1)
         def _():
             pump(step + 1)
         return carry
@@ -419,20 +418,20 @@
         pump(i)
         return carry
 
-    ahead = pp * (layers - EARLY * SUB)
-    lax.fori_loop(2 * (layers - LENT - 1) + pp * (layers + 2 * (LENT - EARLY)), chunks + ahead + 4 * LAG, tail_step, 0)
+    ahead = pp * (layers + SUB - EARLY * SUB)
+    behind = (layers - 1) * SUB - (1 - pp) * sum(c < (layers - 1) * SUB for c in LENT)
+    lax.fori_loop(behind + ahead, chunks + ahead + 4 * LAG, tail_step, 0)
 
     @pl.when(first)
     def _():
-        for n in range(LENT):
+        for n in range(len(LENT)):
             lend(n).wait_send()
-        for n in range(LENT * SUB):
             give_back(n).wait_recv()
-            emit(LENDS[n // SUB] * SUB + n % SUB)
+            emit(LENT[n])
 
     @pl.when(pp == 1)
     def _():
-        for n in range(LENT * SUB):
+        for n in range(len(LENT)):
             give_back(n).wait_send()
 
     down.wait_send()
@@ -454,11 +453,11 @@
     rows = blk // SUB
 
     def step(i, carry):
-        layer, slot = layer_of(pp, i, layers), lax.rem(i, 2)
+        layer, slot = layer_of(pp, i, layers), lax.rem(i, WIDEN_SLOTS)
         puts = (pltpu.make_async_copy(gi_buf.at[slot], gi_hbm.at[layer], gi_sem.at[slot]),
                 pltpu.make_async_copy(go_buf.at[slot], go_hbm.at[layer], go_sem.at[slot]))
 
-        @pl.when(i >= 2)
+        @pl.when(i >= WIDEN_SLOTS)
         def _():
             for put in puts:
                 put.wait()
@@ -477,7 +476,7 @@
         return carry
 
     lax.fori_loop(0, layers, step, 0)
-    for slot in range(2):
+    for slot in range(WIDEN_SLOTS):
         pltpu.make_async_copy(gi_buf.at[slot], gi_hbm.at[slot], gi_sem.at[slot]).wait()
         pltpu.make_async_copy(go_buf.at[slot], go_hbm.at[slot], go_sem.at[slot]).wait()
     put_dx.wait()
@@ -491,7 +490,7 @@
         tokens = dy_in.shape[1]
         blk = ff // 4
         chunks, rows = layers * SUB, blk // SUB
-        room = chunks + LENT * SUB
+        room = chunks + len(LENT)
         dma = pltpu.SemaphoreType.DMA
         flops = 2 * tokens * hidden * ff * layers * 8
         call = pl.pallas_call(
@@ -525,9 +524,9 @@
                 dma((RING,)), dma((RING,)), dma((RING,)), dma((RING,)),
                 dma((RING,)), dma((RING,)), dma((RING,)), dma((RING,)),
                 dma, dma, dma, dma,
-                dma((LENT,)), dma((LENT,)), dma((LENT * SUB,)), dma((LENT * SUB,)), pltpu.SemaphoreType.REGULAR,
+                dma((len(LENT),)), dma((len(LENT),)), dma((len(LENT),)), dma((len(LENT),)), pltpu.SemaphoreType.REGULAR,
             ],
-            compiler_params=pltpu.CompilerParams(collective_id=0, has_side_effects=True, vmem_limit_bytes=67043328 - (35 << 19)),
+            compiler_params=pltpu.CompilerParams(collective_id=0, has_side_effects=True, vmem_limit_bytes=67043328 - (36 << 19)),
             cost_estimate=pl.CostEstimate(flops=flops, bytes_accessed=200 << 20, transcendentals=0),
         )
         own, other, dx, _ = call(w_in, w_out, x_saved, h_saved, dy_in, acc_in, acc_out)
@@ -537,8 +536,9 @@
                        jax.ShapeDtypeStruct((tokens, hidden), BF16)),
             in_specs=[pl.BlockSpec(memory_space=pltpu.VMEM)] * 3,
             out_specs=[pl.BlockSpec(memory_space=pl.ANY)] * 3,
-            scratch_shapes=[pltpu.VMEM((2, hidden, ff), F32), pltpu.VMEM((2, ff, hidden), F32), dma((2,)), dma((2,)), dma],
-            compiler_params=pltpu.CompilerParams(vmem_limit_bytes=12 << 20),
+            scratch_shapes=[pltpu.VMEM((WIDEN_SLOTS, hidden, ff), F32), pltpu.VMEM((WIDEN_SLOTS, ff, hidden), F32),
+                            dma((WIDEN_SLOTS,)), dma((WIDEN_SLOTS,)), dma],
+            compiler_params=pltpu.CompilerParams(vmem_limit_bytes=24 << 20),
         )(own, other, dx)
         return grad_in[None], grad_out[None], dx_out[None]
 

time: 189 us -> 186 us (0.984)
  Pallas kernels: 187 us -> 185 us
where the time goes in v4:
time: 186 us
  Pallas kernels  185 us (99%)
    pallas_call x1, Pallas kernels, device_fn(): call(w_in, w_out, x_saved, h_saved, dy_in, acc_in, acc_out)  174 us
    pallas_call x1, Pallas kernels, device_fn(): pl.pallas_call(functools.partial(widen, layers, blk, 1.0 / replicas), out...  11.1 us

profile of v4, /device:TPU:0, one launch (start us, length us, event | category | flops | bytes accessed | tf_op | source)
XLA Modules:
  0.0 185.7 jit_solution(14313111417220606360)
XLA Ops:
  0.6 173.9 %shard_map.94 = (bf16[36,4,128,256]{3,2,1,0:T(8,128)(2,1)S(1)}, bf16[32,4,128,256]{3,2,1,0:T(8,128)(2,1)S(1)}, bf16[512,256]{1,0:T(8,128)(2,1)S(1)}, bf16[16,512,1024]{2,1,0:T(8,128)(2,1)}) custom-call(bf16[1,16,256,1024]{3,2,1,0:T(8,128)(2,1)} %w1_hbm.1, bf16[1,16,1024,256]{3,2,1,0:T(8,128)(2,1)} %w2_hbm.1, bf16[1,2,16,512,256]{4,3,2,1,0:T(8,128)(2,1)} %x_hbm.1, ...), custom_call_target="tpu_custom_call" | custom-call | flops 34359738368 | bytes 209715200 | tf_op jit(solution)/shard_map/pallas_call | solution.py:532
  174.6 11.1 %shard_map.95 = (f32[16,256,1024]{2,1,0:T(8,128)}, f32[16,1024,256]{2,1,0:T(8,128)}, bf16[512,256]{1,0:T(8,128)(2,1)}) custom-call(bf16[36,4,128,256]{3,2,1,0:T(8,128)(2,1)S(1)} %get-tuple-element.9.own, bf16[32,4,128,256]{3,2,1,0:T(8,128)(2,1)S(1)} %get-tuple-element.10.other, bf16[512,256]{1,0:T(8,128)(2,1)S(1)} %get-tuple-element.11.dx), custom_call_target="tpu_custom_call" | custom-call | tf_op jit(solution)/shard_map/pallas_call | solution.py:533

commit v5 on v4

--- a/solution.py
+++ b/solution.py
@@ -14,9 +14,9 @@
 EARLY = 4
 GAP = 4
 SECOND = 3
-LENDS = {4: (1,), 6: (1,), 8: (1,), 10: (1,)}
+LENDS = {4: (1,), 5: (1,), 6: (1,), 7: (1,)}
 LENT = tuple(m * SUB + t for m, subs in LENDS.items() for t in subs)
-TAKE_AT = 24
+TAKE_AT = 22
 MESH = pl.DeviceIdType.MESH
 ROOT_2_PI = 0.7978845608028654
 CUBIC = 0.044715
@@ -37,6 +37,13 @@
     a = h * s
     q = 2.0 * ROOT_2_PI + (6.0 * ROOT_2_PI * CUBIC) * h2
     return a, s + (a - a * s) * q
+
+
+def twice_slope(h):
+    h2 = h * h
+    t = jnp.tanh(h * (ROOT_2_PI + (ROOT_2_PI * CUBIC) * h2))
+    q = ROOT_2_PI + (3.0 * ROOT_2_PI * CUBIC) * h2
+    return None, (t + ((1.0 - t * t) * h) * q) + 1.0
 
 
 def dot_nt(a, b):
@@ -251,12 +258,13 @@
     pl.semaphore_wait(barrier, 4)
     first_c.wait()
 
-    def chain(c, hs, ws, with_grads):
+    def chain(c, hs, ws, with_grads, slope_of=gelu_slope, scale=1.0):
         total = None
+        c_in = (c * jnp.asarray(scale, c.dtype))
         for f in range(4):
             h = hb[hs, :, cols(f)].astype(F32)
-            a, slope = gelu_slope(h)
-            d = (dot_nt(c, w2b[ws, cols(f), :]) * slope).astype(BF16)
+            a, slope = slope_of(h)
+            d = (dot_nt(c_in, w2b[ws, cols(f), :]) * slope).astype(BF16)
             with_grads(f, a, d)
             back = dot_nt(d, w1b[ws, :, cols(f)])
             total = back if total is None else total + back
@@ -289,6 +297,9 @@
             pl.semaphore_wait(sib_free, 1)
         swap(made).start()
 
+    def down():
+        return remote(c_cur, z_in, z_send, z_recv, (1 - pp, dp))
+
     def chain_step(i, carry):
         layer, slot = layers - 1 - i, lax.rem(i, 2)
         for copy in load_w(layer, slot) + (load_h(0, layer, slot),):
@@ -313,8 +324,12 @@
         def keep(f, a, d):
             dhb[slot, :, cols(f)] = d
 
-        c_cur[...] = chain(c, slot, slot, keep)
+        c_cur[...] = chain(c, slot, slot, keep, twice_slope, 0.5)
         save_dh(layer, slot).start()
+
+        @pl.when((pp == 1) & (i + 1 == layers))
+        def _():
+            down().start()
 
         turn, at = lax.div(i, GAP), lax.rem(i, GAP)
 
@@ -339,11 +354,6 @@
 
     lax.fori_loop(0, layers, chain_step, 0)
 
-    down = pltpu.make_async_remote_copy(c_cur, z_in, z_send, z_recv, device_id=(1 - pp, dp), device_id_type=MESH)
-
-    @pl.when(pp == 1)
-    def _():
-        down.start()
 
     @pl.when(first)
     def _():
@@ -386,7 +396,7 @@
         def _():
             @pl.when(i == 0)
             def _():
-                down.wait_recv()
+                down().wait_recv()
                 c_cur[...] = z_in[...]
 
             c = c_cur[...]
@@ -409,7 +419,7 @@
 
     @pl.when(first)
     def _():
-        down.start()
+        down().start()
 
     for i in (layers - 2, layers - 1):
         swap(i).wait_send()
@@ -434,11 +444,11 @@
         for n in range(len(LENT)):
             give_back(n).wait_send()
 
-    down.wait_send()
+    down().wait_send()
 
     @pl.when(pp == 1)
     def _():
-        down.wait_recv()
+        down().wait_recv()
         dx[...] = z_in[...]
 
     pltpu.make_async_copy(other, other, out_send).wait()

time: 186 us -> 185 us (level)
  no operation moved by 1% of the time
where the time goes in v5:
time: 185 us
  Pallas kernels  184 us (99%)
    pallas_call x1, Pallas kernels, device_fn(): call(w_in, w_out, x_saved, h_saved, dy_in, acc_in, acc_out)  173 us
    pallas_call x1, Pallas kernels, device_fn(): pl.pallas_call(functools.partial(widen, layers, blk, 1.0 / replicas), out...  11.1 us

profile of v5, /device:TPU:0, one launch (start us, length us, event | category | flops | bytes accessed | tf_op | source)
XLA Modules:
  0.0 184.5 jit_solution(4590768702876859942)
XLA Ops:
  0.6 172.8 %shard_map.94 = (bf16[36,4,128,256]{3,2,1,0:T(8,128)(2,1)S(1)}, bf16[32,4,128,256]{3,2,1,0:T(8,128)(2,1)S(1)}, bf16[512,256]{1,0:T(8,128)(2,1)S(1)}, bf16[16,512,1024]{2,1,0:T(8,128)(2,1)}) custom-call(bf16[1,16,256,1024]{3,2,1,0:T(8,128)(2,1)} %w1_hbm.1, bf16[1,16,1024,256]{3,2,1,0:T(8,128)(2,1)} %w2_hbm.1, bf16[1,2,16,512,256]{4,3,2,1,0:T(8,128)(2,1)} %x_hbm.1, ...), custom_call_target="tpu_custom_call" | custom-call | flops 34359738368 | bytes 209715200 | tf_op jit(solution)/shard_map/pallas_call | solution.py:542
  173.4 11.1 %shard_map.95 = (f32[16,256,1024]{2,1,0:T(8,128)}, f32[16,1024,256]{2,1,0:T(8,128)}, bf16[512,256]{1,0:T(8,128)(2,1)}) custom-call(bf16[36,4,128,256]{3,2,1,0:T(8,128)(2,1)S(1)} %get-tuple-element.9.own, bf16[32,4,128,256]{3,2,1,0:T(8,128)(2,1)S(1)} %get-tuple-element.10.other, bf16[512,256]{1,0:T(8,128)(2,1)S(1)} %get-tuple-element.11.dx), custom_call_target="tpu_custom_call" | custom-call | tf_op jit(solution)/shard_map/pallas_call | solution.py:543
